TPU v7x, 32 devices: a whole 2x2x4 slice. The times are simulated.
32 devices in a mesh: dp: 8 (over y, x, core), seq: 4 (over z).
Axes of the slice: x: 2, y: 2, z: 4, core: 2. Of those that a mesh axis runs over, the one named last changes fastest.
Arguments:
- tokens: bfloat16 [16384, 1024], P(('dp', 'seq')), may hold values from -6 to 6
- cotangent: bfloat16 [16384, 1024], P(('dp', 'seq')), may hold values from -6 to 6
- qkv_weight: bfloat16 [1024, 3072], replicated, may hold values from -0.1875 to 0.1875
- proj_weight: bfloat16 [1024, 1024], replicated, may hold values from -0.75 to 0.75
- up_weight: bfloat16 [1024, 4096], replicated, may hold values from -0.1875 to 0.1875
- down_weight: bfloat16 [4096, 1024], replicated, may hold values from -0.09375 to 0.09375
- norm_gains: float32 [2, 1024], replicated, may hold values from 0.5 to 1.5
- biases: float32 [6, 1024], replicated, may hold values from -1.5 to 1.5
- up_bias: float32 [4096], replicated, may hold values from -1.5 to 1.5
- head_slopes: float32 [16], replicated, may hold values from 0.00012207031 to 0.5, as said below
- qkv_moment: float32 [1024, 3072], P(None, 'dp'), may hold values from -1536 to 1536
- proj_moment: float32 [1024, 1024], P(None, 'dp'), may hold values from -1536 to 1536
- up_moment: float32 [1024, 4096], P(None, 'dp'), may hold values from -1536 to 1536
- down_moment: float32 [4096, 1024], P('dp'), may hold values from -1536 to 1536
- gains_moment: float32 [2, 1024], P(None, 'dp'), may hold values from -768 to 768
- biases_moment: float32 [6, 1024], P(None, 'dp'), may hold values from -768 to 768
- upbias_moment: float32 [4096], P('dp'), may hold values from -768 to 768
Outputs:
- block_out: bfloat16 [16384, 1024], P(('dp', 'seq'))
- tokens_grad: float32 [16384, 1024], P(('dp', 'seq'))
- qkv_grad: float32 [1024, 3072], P(None, 'dp')
- proj_grad: float32 [1024, 1024], P(None, 'dp')
- up_grad: float32 [1024, 4096], P(None, 'dp')
- down_grad: float32 [4096, 1024], P('dp')
- gains_grad: float32 [2, 1024], P(None, 'dp')
- biases_grad: float32 [6, 1024], P(None, 'dp')
- upbias_grad: float32 [4096], P('dp')
- qkv_state: float32 [1024, 3072], P(None, 'dp')
- proj_state: float32 [1024, 1024], P(None, 'dp')
- up_state: float32 [1024, 4096], P(None, 'dp')
- down_state: float32 [4096, 1024], P('dp')
- gains_state: float32 [2, 1024], P(None, 'dp')
- biases_state: float32 [6, 1024], P(None, 'dp')
- upbias_state: float32 [4096], P('dp')
- qkv_new: float32 [1024, 3072], P(None, 'dp')
- proj_new: float32 [1024, 1024], P(None, 'dp')
- up_new: float32 [1024, 4096], P(None, 'dp')
- down_new: float32 [4096, 1024], P('dp')
- gains_new: float32 [2, 1024], P(None, 'dp')
- biases_new: float32 [6, 1024], P(None, 'dp')
- upbias_new: float32 [4096], P('dp')
Inputs may be any that keep to these rules, and one draw needn't show every extreme that they name: `head_slopes`: one positive slope a head.
All inputs are finite; a program needn't handle non-finite values.
Results may differ from a plain program's by a relative error of at most 0.025.
Values may be sent and summed in bfloat16 or wider, within the bound.
A program may use at most 256 MiB of HBM per device.

v0:
```python
import math
import jax
import jax.numpy as jnp
from jax import lax
from jax.sharding import PartitionSpec as P

NS_ITERS = 5
MOMENTUM = 0.9
RATE_MATRIX = 0.2
RATE_VECTOR = 0.0015
NORM_EPS = 1e-05
ORTHO_EPS = 1e-07
COEF_A = 2.0
COEF_B = -1.0
GELU_C = 0.7978845608028654
MASKED = -1e30


def norm_forward(values, gain_row, offset):
    center = values - jnp.mean(values, axis=-1, keepdims=True)
    inv_scale = lax.rsqrt(jnp.mean(center * center, axis=-1, keepdims=True) + NORM_EPS)
    unit_values = center * inv_scale
    return (unit_values * gain_row + offset, unit_values, inv_scale)


def norm_backward(upstream, unit_values, inv_scale, gain_row):
    scaled = upstream * gain_row
    inner_sum = jnp.mean(scaled * unit_values, axis=-1, keepdims=True)
    input_grad = inv_scale * (
        scaled - jnp.mean(scaled, axis=-1, keepdims=True) - unit_values * inner_sum
    )
    return (input_grad, jnp.sum(upstream * unit_values, axis=0), jnp.sum(upstream, axis=0))


def gelu_tanh(values):
    return 0.5 * values * (1.0 + jnp.tanh(GELU_C * (values + 0.044715 * values * values * values)))


def gelu_slope(values):
    tangent = jnp.tanh(GELU_C * (values + 0.044715 * values * values * values))
    return 0.5 * (1.0 + tangent) + 0.5 * values * (1.0 - tangent * tangent) * GELU_C * (
        1.0 + 3.0 * 0.044715 * values * values
    )


def contract_rows(left, right):
    return lax.dot_general(
        left, right, (((0,), (0,)), ((), ())), preferred_element_type=jnp.float32
    )


def contract_cols(left, right):
    return lax.dot_general(
        left, right, (((1,), (1,)), ((), ())), preferred_element_type=jnp.float32
    )


def split_heads(matrix, groups):
    row_count = matrix.shape[0]
    return jnp.moveaxis(matrix.reshape(row_count, groups, 2, -1), 1, 0)


def join_heads(stacked):
    row_count = stacked.shape[1]
    return jnp.moveaxis(stacked, 0, 1).reshape(row_count, -1)


def score_block(query_g, key_g, slope_g, distance, allowed):
    scale = 1.0 / math.sqrt(query_g.shape[-1])
    scores = jnp.einsum("qhd,khd->hqk", query_g, key_g, preferred_element_type=jnp.float32) * scale
    scores = scores - slope_g[:, None, None] * distance[None]
    return jnp.where(allowed[None], scores, MASKED)


def group_forward(items, distance, allowed):
    query_g, key_g, value_g, slope_g = items
    scores = score_block(query_g, key_g, slope_g, distance, allowed)
    peak_score = jnp.max(scores, axis=-1, keepdims=True)
    log_total = peak_score + jnp.log(jnp.sum(jnp.exp(scores - peak_score), axis=-1, keepdims=True))
    soft_weights = jnp.exp(scores - log_total).astype(jnp.bfloat16)
    attended = jnp.einsum("hqk,khd->qhd", soft_weights, value_g, preferred_element_type=jnp.float32)
    return (attended, log_total[..., 0])


def group_backward(items, distance, allowed):
    query_g, key_g, value_g, slope_g, log_total, upstream_g = items
    scale = 1.0 / math.sqrt(query_g.shape[-1])
    scores = score_block(query_g, key_g, slope_g, distance, allowed)
    chances = jnp.exp(scores - log_total[..., None])
    soft_weights = chances.astype(jnp.bfloat16)
    soft_grad = jnp.einsum("qhd,khd->hqk", upstream_g, value_g, preferred_element_type=jnp.float32)
    inner_sum = jnp.sum(soft_grad * chances, axis=-1, keepdims=True)
    score_grad = (chances * (soft_grad - inner_sum)).astype(jnp.bfloat16)
    query_grad = (
        jnp.einsum("hqk,khd->qhd", score_grad, key_g, preferred_element_type=jnp.float32) * scale
    ).astype(jnp.bfloat16)
    key_grad = (
        jnp.einsum("hqk,qhd->khd", score_grad, query_g, preferred_element_type=jnp.float32) * scale
    )
    value_grad = jnp.einsum(
        "hqk,qhd->khd", soft_weights, upstream_g, preferred_element_type=jnp.float32
    )
    return (query_grad, key_grad, value_grad)


def on_device(
    tokens,
    cotangent,
    qkv_weight,
    proj_weight,
    up_weight,
    down_weight,
    norm_gains,
    biases,
    up_bias,
    head_slopes,
    qkv_moment,
    proj_moment,
    up_moment,
    down_moment,
    gains_moment,
    biases_moment,
    upbias_moment,
):
    row_count, model_width = tokens.shape
    groups = head_slopes.shape[0] // 2
    seq_length = row_count * lax.axis_size("seq")
    positions = lax.axis_index("seq") * row_count + jnp.arange(row_count, dtype=jnp.int32)
    key_index = jnp.arange(seq_length, dtype=jnp.int32)
    distance = (positions[:, None] - key_index[None, :]).astype(jnp.float32)
    allowed = key_index[None, :] <= positions[:, None]
    slopes = head_slopes.reshape(groups, 2)
    inputs = tokens.astype(jnp.float32)
    normed_one, unit_one, scale_one = norm_forward(inputs, norm_gains[0], biases[0])
    normed_one = normed_one.astype(jnp.bfloat16)
    mixed = jnp.dot(normed_one, qkv_weight, preferred_element_type=jnp.float32)
    queries = (mixed[:, :model_width] + biases[1]).astype(jnp.bfloat16)
    key_part = mixed[:, model_width : 2 * model_width].astype(jnp.bfloat16)
    value_part = (mixed[:, 2 * model_width :] + biases[2]).astype(jnp.bfloat16)
    key_rows, value_rows = (
        lax.all_gather(key_part, "seq", axis=0, tiled=True),
        lax.all_gather(value_part, "seq", axis=0, tiled=True),
    )
    query_groups = split_heads(queries, groups)
    key_groups = split_heads(key_rows, groups)
    value_groups = split_heads(value_rows, groups)

    def forward_group(items):
        return group_forward(items, distance, allowed)

    attended, log_totals = lax.map(forward_group, (query_groups, key_groups, value_groups, slopes))
    mixed_heads = join_heads(attended).astype(jnp.bfloat16)
    middle = (
        inputs + jnp.dot(mixed_heads, proj_weight, preferred_element_type=jnp.float32) + biases[3]
    )
    normed_two, unit_two, scale_two = norm_forward(middle, norm_gains[1], biases[4])
    normed_two = normed_two.astype(jnp.bfloat16)
    before = jnp.dot(normed_two, up_weight, preferred_element_type=jnp.float32) + up_bias
    hidden = gelu_tanh(before).astype(jnp.bfloat16)
    block_out = (
        middle + jnp.dot(hidden, down_weight, preferred_element_type=jnp.float32) + biases[5]
    ).astype(jnp.bfloat16)
    upstream = cotangent.astype(jnp.float32)
    down_grad = contract_rows(cotangent, hidden)
    hidden_grad = contract_cols(cotangent, down_weight)
    before_grad = (hidden_grad * gelu_slope(before)).astype(jnp.bfloat16)
    up_grad = contract_rows(normed_two, before_grad)
    normed_two_grad = contract_cols(before_grad, up_weight)
    middle_back, gain_two_grad, offset_two_grad = norm_backward(
        normed_two_grad, unit_two, scale_two, norm_gains[1]
    )
    middle_grad = upstream + middle_back
    branch_grad = middle_grad.astype(jnp.bfloat16)
    proj_grad = contract_rows(mixed_heads, branch_grad)
    heads_grad = contract_cols(branch_grad, proj_weight).astype(jnp.bfloat16)

    def backward_group(items):
        return group_backward(items, distance, allowed)

    query_grad, key_grad, value_grad = lax.map(
        backward_group,
        (
            query_groups,
            key_groups,
            value_groups,
            slopes,
            log_totals,
            split_heads(heads_grad, groups),
        ),
    )
    query_grad = join_heads(query_grad)
    key_sum, value_sum = (
        lax.psum_scatter(
            join_heads(key_grad).astype(jnp.bfloat16), "seq", scatter_dimension=0, tiled=True
        ).astype(jnp.float32),
        lax.psum_scatter(
            join_heads(value_grad).astype(jnp.bfloat16), "seq", scatter_dimension=0, tiled=True
        ).astype(jnp.float32),
    )
    key_low = key_sum.astype(jnp.bfloat16)
    value_low = value_sum.astype(jnp.bfloat16)
    mixed_grad = jnp.concatenate([query_grad, key_low, value_low], axis=1)
    qkv_grad = contract_rows(normed_one, mixed_grad)
    normed_one_grad = contract_cols(mixed_grad, qkv_weight)
    input_back, gain_one_grad, offset_one_grad = norm_backward(
        normed_one_grad, unit_one, scale_one, norm_gains[0]
    )
    tokens_grad = middle_grad + input_back
    gains_grad = jnp.stack([gain_one_grad, gain_two_grad])
    biases_grad = jnp.stack(
        [
            offset_one_grad,
            jnp.sum(query_grad.astype(jnp.float32), axis=0),
            jnp.sum(value_low.astype(jnp.float32), axis=0),
            jnp.sum(branch_grad.astype(jnp.float32), axis=0),
            offset_two_grad,
            jnp.sum(upstream, axis=0),
        ]
    )
    upbias_grad = jnp.sum(before_grad.astype(jnp.float32), axis=0)[None]
    qkv_part, proj_part, up_part, down_part, gains_part, biases_part, upbias_part = (
        lax.psum_scatter(
            qkv_grad.astype(jnp.bfloat16), "dp", scatter_dimension=1, tiled=True
        ).astype(jnp.float32),
        lax.psum_scatter(
            proj_grad.astype(jnp.bfloat16), "dp", scatter_dimension=1, tiled=True
        ).astype(jnp.float32),
        lax.psum_scatter(
            up_grad.astype(jnp.bfloat16), "dp", scatter_dimension=1, tiled=True
        ).astype(jnp.float32),
        lax.psum_scatter(
            down_grad.astype(jnp.bfloat16), "dp", scatter_dimension=1, tiled=True
        ).astype(jnp.float32),
        lax.psum_scatter(
            gains_grad.astype(jnp.bfloat16), "dp", scatter_dimension=1, tiled=True
        ).astype(jnp.float32),
        lax.psum_scatter(
            biases_grad.astype(jnp.bfloat16), "dp", scatter_dimension=1, tiled=True
        ).astype(jnp.float32),
        lax.psum_scatter(
            upbias_grad.astype(jnp.bfloat16), "dp", scatter_dimension=1, tiled=True
        ).astype(jnp.float32),
    )
    qkv_sum, proj_sum, up_sum, down_sum, gains_sum, biases_sum, upbias_sum = (
        lax.psum(qkv_part.astype(jnp.bfloat16), "seq").astype(jnp.float32),
        lax.psum(proj_part.astype(jnp.bfloat16), "seq").astype(jnp.float32),
        lax.psum(up_part.astype(jnp.bfloat16), "seq").astype(jnp.float32),
        lax.psum(down_part.astype(jnp.bfloat16), "seq").astype(jnp.float32),
        lax.psum(gains_part.astype(jnp.bfloat16), "seq").astype(jnp.float32),
        lax.psum(biases_part.astype(jnp.bfloat16), "seq").astype(jnp.float32),
        lax.psum(upbias_part.astype(jnp.bfloat16), "seq").astype(jnp.float32),
    )
    qkv_state = MOMENTUM * qkv_moment + qkv_sum
    proj_state = MOMENTUM * proj_moment + proj_sum
    up_state = MOMENTUM * up_moment + up_sum
    down_oriented = MOMENTUM * down_moment.T + down_sum
    gains_state = MOMENTUM * gains_moment + gains_sum
    biases_state = MOMENTUM * biases_moment + biases_sum
    upbias_state = MOMENTUM * upbias_moment + upbias_sum[0]
    oriented = (qkv_state, proj_state, up_state, down_oriented)
    pad_width = max((member.shape[1] for member in oriented))
    stacked = jnp.stack(
        [
            jnp.pad(member.astype(jnp.bfloat16), ((0, 0), (0, pad_width - member.shape[1])))
            for member in oriented
        ]
    )
    owned_block = lax.dynamic_index_in_dim(stacked, lax.axis_index("seq"), 0, keepdims=False)
    iterate = owned_block
    for iteration in range(NS_ITERS):
        gram = lax.psum(contract_cols(iterate, iterate).astype(jnp.bfloat16), "dp").astype(
            jnp.float32
        )
        if iteration == 0:
            factor = 1.0 / (jnp.sqrt(jnp.trace(gram)) + ORTHO_EPS)
            square = gram * factor * factor
            iterate = (owned_block.astype(jnp.float32) * factor).astype(jnp.bfloat16)
        else:
            square = gram
        square_low = square.astype(jnp.bfloat16)
        iterate = (
            COEF_A * iterate.astype(jnp.float32)
            + COEF_B * jnp.dot(square_low, iterate, preferred_element_type=jnp.float32)
        ).astype(jnp.bfloat16)
    shared = lax.all_gather(iterate[None], "seq", axis=0, tiled=True)

    def step_of(slot_number, column_count, whole_shape):
        return (
            -RATE_MATRIX
            * math.sqrt(max(whole_shape[0], whole_shape[1]))
            * shared[slot_number][:, :column_count].astype(jnp.float32)
        )

    dp_index = lax.axis_index("dp")

    def own_cols(matrix, count):
        return lax.dynamic_slice_in_dim(matrix, dp_index * count, count, 1).astype(jnp.float32)

    qkv_new = own_cols(qkv_weight, qkv_state.shape[1]) + step_of(
        0, qkv_state.shape[1], qkv_weight.shape
    )
    proj_new = own_cols(proj_weight, proj_state.shape[1]) + step_of(
        1, proj_state.shape[1], proj_weight.shape
    )
    up_new = own_cols(up_weight, up_state.shape[1]) + step_of(2, up_state.shape[1], up_weight.shape)
    down_count = down_oriented.shape[1]
    down_rows = lax.dynamic_slice_in_dim(down_weight, dp_index * down_count, down_count, 0).astype(
        jnp.float32
    )
    down_new = down_rows + step_of(3, down_count, down_weight.shape).T
    gains_new = own_cols(norm_gains, gains_state.shape[1]) - RATE_VECTOR * gains_state
    biases_new = own_cols(biases, biases_state.shape[1]) - RATE_VECTOR * biases_state
    upbias_count = upbias_state.shape[0]
    upbias_new = (
        lax.dynamic_slice_in_dim(up_bias, dp_index * upbias_count, upbias_count, 0)
        - RATE_VECTOR * upbias_state
    )
    return (
        block_out,
        tokens_grad,
        qkv_sum,
        proj_sum,
        up_sum,
        down_sum.T,
        gains_sum,
        biases_sum,
        upbias_sum[0],
        qkv_state,
        proj_state,
        up_state,
        down_oriented.T,
        gains_state,
        biases_state,
        upbias_state,
        qkv_new,
        proj_new,
        up_new,
        down_new,
        gains_new,
        biases_new,
        upbias_new,
    )


def solution(mesh):
    placed = (
        P(("dp", "seq"), None),
        P(("dp", "seq"), None),
        P(),
        P(),
        P(),
        P(),
        P(),
        P(),
        P(),
        P(),
        P(None, "dp"),
        P(None, "dp"),
        P(None, "dp"),
        P("dp", None),
        P(None, "dp"),
        P(None, "dp"),
        P("dp"),
    )
    return jax.shard_map(
        on_device,
        mesh=mesh,
        in_specs=placed,
        out_specs=(
            P(("dp", "seq"), None),
            P(("dp", "seq"), None),
            P(None, "dp"),
            P(None, "dp"),
            P(None, "dp"),
            P("dp", None),
            P(None, "dp"),
            P(None, "dp"),
            P("dp"),
            P(None, "dp"),
            P(None, "dp"),
            P(None, "dp"),
            P("dp", None),
            P(None, "dp"),
            P(None, "dp"),
            P("dp"),
            P(None, "dp"),
            P(None, "dp"),
            P(None, "dp"),
            P("dp", None),
            P(None, "dp"),
            P(None, "dp"),
            P("dp"),
        ),
        check_vma=False,
    )
```

profile of v0, /device:TPU:0, one launch (start us, length us, event | category | flops | bytes accessed | tf_op | source)
XLA Modules:
  0.0 1661.3 jit_solution(17056713743389701598)
XLA Ops:
  12.8 6.1 fusion.105
  26.7 78.8 %all-gather.5.cloned.1.call-done = bf16[2048,1024]{1,0:T(8,128)(2,1)} async-done(((bf16[512,1024]{1,0:T(8,128)(2,1)}), bf16[2048,1024]{1,0:T(8,128)(2,1)}) %all-gather.5.cloned.1.call-update) | async-done | bytes 4194320 | tf_op jit(solution)/shard_map/all_gather | solution.py:142
  105.5 6.5 copy.60
  112.0 74.9 %all-gather.7.cloned.1.call-done = bf16[2048,1024]{1,0:T(8,128)(2,1)} async-done(((bf16[512,1024]{1,0:T(8,128)(2,1)}), bf16[2048,1024]{1,0:T(8,128)(2,1)}) %all-gather.7.cloned.1.call-update) | async-done | bytes 4194320 | tf_op jit(solution)/shard_map/all_gather | solution.py:141
  186.9 6.5 copy.62
  193.4 102.7 %while.30 = (s32[]{:T(128)}, bf16[8,512,2,64]{1,3,2,0:T(8,128)(2,1)}, f32[8,2,512]{2,1,0:T(2,128)S(1)}, bf16[8,2048,2,64]{1,3,2,0:T(8,128)(2,1)}, bf16[8,512,2,6...) while((s32[]{:T(128)}, ...), condition=%wide.region_5.6_spmd.clone.clone, body=%wide.region_2.5_spmd.clone.clone.sunk | while | flops 575667200 | bytes 47618196 | solution.py:151
  299.1 10.7 fusion.107
  309.8 13.6 fusion.113
  323.4 5.7 multiply_reduce_fusion.1
  334.6 222.8 %while.31 = (s32[]{:T(128)}, bf16[8,512,2,64]{1,3,2,0:T(8,128)(2,1)}, bf16[8,2048,2,64]{1,3,2,0:T(8,128)(2,1)}, bf16[8,2048,2,64]{1,3,2,0:T(8,128)(2,1)}, bf16[8...) while((s32[]{:T(128)}, ...), condition=%wide.region_12.13_spmd.clone.clone, body=%wide.region_10.12_spmd.clone.clone.sunk | while | flops 1368783872 | bytes 144864496 | solution.py:180
  343.3 5.7 multiply_reduce_fusion.7
  349.0 6.6 multiply_convert_fusion.7
  371.1 5.7 multiply_reduce_fusion.7
  376.8 6.6 multiply_convert_fusion.7
  398.9 5.7 multiply_reduce_fusion.7
  404.6 6.6 multiply_convert_fusion.7
  426.7 5.7 multiply_reduce_fusion.7
  432.4 6.6 multiply_convert_fusion.7
  454.5 5.7 multiply_reduce_fusion.7
  460.3 6.6 multiply_convert_fusion.7
  482.4 5.7 multiply_reduce_fusion.7
  488.1 6.6 multiply_convert_fusion.7
  510.2 5.7 multiply_reduce_fusion.7
  515.9 6.6 multiply_convert_fusion.7
  538.0 5.7 multiply_reduce_fusion.7
  543.7 6.6 multiply_convert_fusion.7
  566.6 66.1 %reduce-scatter.20.cloned.1.call-done = bf16[512,1024]{0,1:T(8,128)(2,1)} async-done(((bf16[2048,1024]{0,1:T(8,128)(2,1)}), bf16[512,1024]{0,1:T(8,128)(2,1)}) %reduce-scatter.20.cloned.1.call-update) | async-done | bytes 1048592 | tf_op jit(solution)/shard_map/reduce_scatter | solution.py:193
  632.7 79.5 %reduce-scatter.22.cloned.1.call-done = bf16[512,1024]{0,1:T(8,128)(2,1)} async-done(((bf16[2048,1024]{0,1:T(8,128)(2,1)}), bf16[512,1024]{0,1:T(8,128)(2,1)}) %reduce-scatter.22.cloned.1.call-update) | async-done | bytes 1048592 | tf_op jit(solution)/shard_map/reduce_scatter | solution.py:196
  712.2 8.1 convolution_convert_fusion.1
  720.3 8.6 copy.71
  730.2 11.4 convert_bitcast_fusion
  743.2 9.2 convolution_convert_fusion
  759.4 63.2 %reduce-scatter.28.cloned.1.call-done = bf16[384,1024]{1,0:T(8,128)(2,1)} async-done(((bf16[3072,1024]{1,0:T(8,128)(2,1)}), bf16[384,1024]{1,0:T(8,128)(2,1)}) %reduce-scatter.28.cloned.1.call-update) | async-done | bytes 786448
  824.9 72.5 %reduce-scatter.26.cloned.1.call-done = bf16[1024,512]{1,0:T(8,128)(2,1)} async-done(((bf16[1024,4096]{1,0:T(8,128)(2,1)}), bf16[1024,512]{1,0:T(8,128)(2,1)}) %reduce-scatter.26.cloned.1.call-update) | async-done | bytes 1048592 | tf_op jit(solution)/shard_map/reduce_scatter | solution.py:231
  897.4 74.8 %reduce-scatter.24.cloned.1.call-done = bf16[1024,512]{1,0:T(8,128)(2,1)} async-done(((bf16[1024,4096]{1,0:T(8,128)(2,1)}), bf16[1024,512]{1,0:T(8,128)(2,1)}) %reduce-scatter.24.cloned.1.call-update) | async-done | bytes 1048592 | tf_op jit(solution)/shard_map/reduce_scatter | solution.py:228
  975.1 121.9 %all-reduce.21.cloned.1.call-done = (bf16[1024,384]{1,0:T(8,128)(2,1)}, bf16[1024,128]{1,0:T(8,128)(2,1)}, bf16[1024,512]{1,0:T(8,128)(2,1)}, bf16[1024,512]{1,0:T(8,128)(2,1)}) async-done(((bf16[1024,384]{1,0:T(8,128)(2,1)}, bf16[1024,128]{1,0:T(8,128)(2,1)}, bf16[1024,512]{1,0:T(8,128)(2,1)}, bf16[1024,512]{1,0:T(8,128)(2,1)}), (bf16[1024,384]{1,0:T(8,128)(2,1)}, bf16[1024,128]{1,0:T(8,128)(2,1)}, ...) | async-done | bytes 3145744 | tf_op jit(solution)/shard_map/psum | solution.py:245
  1112.3 60.9 %all-reduce.11.cloned.1.call-done = bf16[1024,1024]{1,0:T(8,128)(2,1)} async-done(((bf16[1024,1024]{1,0:T(8,128)(2,1)}), bf16[1024,1024]{1,0:T(8,128)(2,1)}) %all-reduce.11.cloned.1.call-update) | async-done | bytes 2097168 | tf_op jit(solution)/shard_map/psum | solution.py:271
  1183.4 60.9 %all-reduce.13.cloned.1.call-done = bf16[1024,1024]{1,0:T(8,128)(2,1)} async-done(((bf16[1024,1024]{1,0:T(8,128)(2,1)}), bf16[1024,1024]{1,0:T(8,128)(2,1)}) %all-reduce.13.cloned.1.call-update) | async-done | bytes 2097168 | tf_op jit(solution)/shard_map/psum | solution.py:271
  1251.4 60.9 %all-reduce.15.cloned.1.call-done = bf16[1024,1024]{1,0:T(8,128)(2,1)} async-done(((bf16[1024,1024]{1,0:T(8,128)(2,1)}), bf16[1024,1024]{1,0:T(8,128)(2,1)}) %all-reduce.15.cloned.1.call-update) | async-done | bytes 2097168 | tf_op jit(solution)/shard_map/psum | solution.py:271
  1319.5 60.9 %all-reduce.17.cloned.1.call-done = bf16[1024,1024]{1,0:T(8,128)(2,1)} async-done(((bf16[1024,1024]{1,0:T(8,128)(2,1)}), bf16[1024,1024]{1,0:T(8,128)(2,1)}) %all-reduce.17.cloned.1.call-update) | async-done | bytes 2097168 | tf_op jit(solution)/shard_map/psum | solution.py:271
  1389.4 9.4 fusion.80
  1404.0 44.5 %all-reduce.19.cloned.1.call-done = bf16[1024,1024]{1,0:T(8,128)(2,1)} async-done(((bf16[1024,1024]{1,0:T(8,128)(2,1)}), bf16[1024,1024]{1,0:T(8,128)(2,1)}) %all-reduce.19.cloned.1.call-update) | async-done | bytes 2097168 | tf_op jit(solution)/shard_map/psum | solution.py:271
  1457.5 12.6 add_convert_fusion.5
  1470.1 17.1 %reduce-scatter.36.cloned.1.call-done = bf16[512,1]{1,0:T(8,128)(2,1)} async-done(((bf16[4096,1]{1,0:T(8,128)(2,1)}), bf16[512,1]{1,0:T(8,128)(2,1)}) %reduce-scatter.36.cloned.1.call-update) | async-done | bytes 1040
  1492.5 31.8 %reduce-scatter.32.cloned.1.call-done = bf16[128,2]{1,0:T(8,128)(2,1)} async-done(((bf16[1024,2]{1,0:T(8,128)(2,1)}), bf16[128,2]{1,0:T(8,128)(2,1)}) %reduce-scatter.32.cloned.1.call-update) | async-done | bytes 528
  1525.2 35.7 %reduce-scatter.34.cloned.1.call-done = bf16[128,6]{1,0:T(8,128)(2,1)} async-done(((bf16[1024,6]{1,0:T(8,128)(2,1)}), bf16[128,6]{1,0:T(8,128)(2,1)}) %reduce-scatter.34.cloned.1.call-update) | async-done | bytes 1552
  1561.7 11.8 all-reduce.2
  1584.4 58.7 %all-gather.9.cloned.1.call-done = bf16[4096,512]{1,0:T(8,128)(2,1)} async-done(((bf16[1024,512]{1,0:T(8,128)(2,1)}), bf16[4096,512]{1,0:T(8,128)(2,1)}) %all-gather.9.cloned.1.call-update) | async-done | bytes 4194320 | tf_op jit(solution)/shard_map/all_gather | solution.py:285
  (385 shorter events, 362.5 us)
Async XLA Ops:
  7.2 98.3 %all-gather.5.cloned.1.call-start = ((), (), s32[]{:S(2)}) async-start(), calls=%async_computation.9 | async-start | bytes 5242880 | tf_op jit(solution)/shard_map/all_gather | solution.py:142
  8.7 10.2 copy-start.24
  10.3 8.5 copy-start.31
  11.1 7.7 copy-start.26
  12.7 6.1 copy-start.36
  12.8 286.3 %copy-start.34 = (f32[1,1024]{1,0:T(1,128)}, f32[1,1024]{1,0:T(1,128)S(1)}, u32[]{:S(2)}) copy-start(f32[1,1024]{1,0:T(1,128)S(1)} %get-tuple-element.393) | copy-start | bytes 12292
  21.9 165.0 %all-gather.7.cloned.1.call-start = ((), (), s32[]{:S(2)}) async-start(), calls=%async_computation.10 | async-start | bytes 5242880 | tf_op jit(solution)/shard_map/all_gather | solution.py:141
  24.7 608.1 %reduce-scatter.20.cloned.1.call-start = ((), (), s32[]{:S(2)}) async-start(), calls=%async_computation.11 | async-start | bytes 5242880 | tf_op jit(solution)/shard_map/reduce_scatter | solution.py:193
  193.4 102.7 %copy-start.3 = (bf16[512,1024]{1,0:T(8,128)(2,1)S(1)}, bf16[512,1024]{1,0:T(8,128)(2,1)}, u32[]{:S(2)}) copy-start(bf16[512,1024]{1,0:T(8,128)(2,1)} %param.21) | copy-start | bytes 3145732
  193.4 102.7 %copy-start.14 = (bf16[1024,1024]{1,0:T(8,128)(2,1)S(1)}, bf16[1024,1024]{1,0:T(8,128)(2,1)}, u32[]{:S(2)}) copy-start(bf16[1024,1024]{1,0:T(8,128)(2,1)} %param.24) | copy-start | bytes 6291460
  298.6 30.4 %copy-start.1 = (f32[512,1024]{1,0:T(8,128)}, f32[512,1024]{1,0:T(8,128)S(1)}, u32[]{:S(2)}) copy-start(f32[512,1024]{1,0:T(8,128)S(1)} %get-tuple-element.402) | copy-start | bytes 6291460
  299.0 10.8 copy-start.17
  299.0 10.8 copy-start.44
  299.0 24.3 %slice-start = ((s8[8388608]{0:T(1024)(128)(4,1)}), s8[4194304]{0:T(1024)(128)(4,1)S(1)}, s32[]{:S(2)}) async-start(s8[8388608]{0:T(1024)(128)(4,1)} %bitcast.226), calls=%async_computation.27 | async-start | bytes 8388608
  309.8 13.6 slice-start.1
  323.4 5.7 copy-start.49
  451.1 3.4 copy-start
  478.9 3.4 copy-start
  557.4 154.8 %reduce-scatter.22.cloned.1.call-start = ((), (), s32[]{:S(2)}) async-start(), calls=%async_computation.12 | async-start | bytes 5242880 | tf_op jit(solution)/shard_map/reduce_scatter | solution.py:196
  558.0 199.6 %reduce-scatter.30.cloned.1.call-start = ((), (), s32[]{:S(2)}) async-start(), calls=%async_computation.22 | async-start | bytes 2359296
  561.8 150.4 %copy-start.4 = (bf16[512,1024]{1,0:T(8,128)(2,1)S(1)}, bf16[512,1024]{1,0:T(8,128)(2,1)}, u32[]{:S(2)}) copy-start(bf16[512,1024]{1,0:T(8,128)(2,1)} %param.21) | copy-start | bytes 3145732
  561.8 150.4 %copy-start.19 = (bf16[8,512,2,64]{1,3,2,0:T(8,128)(2,1)S(1)}, bf16[8,512,2,64]{1,3,2,0:T(8,128)(2,1)}, u32[]{:S(2)}) copy-start(bf16[8,512,2,64]{1,3,2,0:T(8,128)(2,1)} %get-tuple-element.137) | copy-start | bytes 3145732
  561.8 150.4 %copy-start.25 = (f32[512]{0:T(512)S(1)}, f32[512]{0:T(512)}, u32[]{:S(2)}) copy-start(f32[512]{0:T(512)} %copy-done.24) | copy-start | bytes 6148
  561.8 150.4 %copy-start.27 = (f32[1,1024]{1,0:T(1,128)S(1)}, f32[1,1024]{1,0:T(1,128)}, u32[]{:S(2)}) copy-start(f32[1,1024]{1,0:T(1,128)} %copy-done.26) | copy-start | bytes 12292
  561.8 150.4 %copy-start.32 = (f32[512]{0:T(512)S(1)}, f32[512]{0:T(512)}, u32[]{:S(2)}) copy-start(f32[512]{0:T(512)} %copy-done.31) | copy-start | bytes 6148
  561.8 150.4 %copy-start.37 = (f32[1,1024]{1,0:T(1,128)S(1)}, f32[1,1024]{1,0:T(1,128)}, u32[]{:S(2)}) copy-start(f32[1,1024]{1,0:T(1,128)} %copy-done.36) | copy-start | bytes 12292
  566.1 256.4 %reduce-scatter.28.cloned.1.call-start = ((), (), s32[]{:S(2)}) async-start(), calls=%async_computation.21 | async-start | bytes 7077888
  729.0 168.4 %reduce-scatter.26.cloned.1.call-start = ((), (), s32[]{:S(2)}) async-start(), calls=%async_computation.14 | async-start | bytes 9437184 | tf_op jit(solution)/shard_map/reduce_scatter | solution.py:231
  741.6 230.6 %reduce-scatter.24.cloned.1.call-start = ((), (), s32[]{:S(2)}) async-start(), calls=%async_computation.13 | async-start | bytes 9437184 | tf_op jit(solution)/shard_map/reduce_scatter | solution.py:228
  752.5 344.6 %all-reduce.21.cloned.1.call-start = ((), (), s32[]{:S(2)}) async-start(), calls=%async_computation.26 | async-start | bytes 6291456 | tf_op jit(solution)/shard_map/psum | solution.py:245
  972.2 200.9 %all-reduce.11.cloned.1.call-start = ((), (), s32[]{:S(2)}) async-start(), calls=%async_computation.15 | async-start | bytes 4194304 | tf_op jit(solution)/shard_map/psum | solution.py:271
  1112.2 132.2 %all-reduce.13.cloned.1.call-start = ((), (), s32[]{:S(2)}) async-start(), calls=%async_computation.16 | async-start | bytes 4194304 | tf_op jit(solution)/shard_map/psum | solution.py:271
  1183.4 129.0 %all-reduce.15.cloned.1.call-start = ((), (), s32[]{:S(2)}) async-start(), calls=%async_computation.17 | async-start | bytes 4194304 | tf_op jit(solution)/shard_map/psum | solution.py:271
  1251.4 129.0 %all-reduce.17.cloned.1.call-start = ((), (), s32[]{:S(2)}) async-start(), calls=%async_computation.18 | async-start | bytes 4194304 | tf_op jit(solution)/shard_map/psum | solution.py:271
  1319.4 129.1 %all-reduce.19.cloned.1.call-start = ((), (), s32[]{:S(2)}) async-start(), calls=%async_computation.19 | async-start | bytes 4194304 | tf_op jit(solution)/shard_map/psum | solution.py:271
  1387.5 99.7 %reduce-scatter.36.cloned.1.call-start = ((), (), s32[]{:S(2)}) async-start(), calls=%async_computation.25 | async-start | bytes 1179648
  1389.1 12.2 copy-start.39
  1389.2 12.2 copy-start.30
  1389.2 12.2 copy-start.29
  1389.2 135.2 %reduce-scatter.32.cloned.1.call-start = ((), (), s32[]{:S(2)}) async-start(), calls=%async_computation.23 | async-start | bytes 294912
  1399.8 161.1 %reduce-scatter.34.cloned.1.call-start = ((), (), s32[]{:S(2)}) async-start(), calls=%async_computation.24 | async-start | bytes 294912
  1403.9 239.2 %all-gather.9.cloned.1.call-start = ((), (), s32[]{:S(2)}) async-start(), calls=%async_computation.20 | async-start | bytes 5242880 | tf_op jit(solution)/shard_map/all_gather | solution.py:285
  1452.9 4.6 copy-start.33
  1488.2 85.3 %copy-start.42 = (f32[2,128]{1,0:T(2,128)S(1)}, f32[2,128]{1,0:T(2,128)}, u32[]{:S(2)}) copy-start(f32[2,128]{1,0:T(2,128)} %param.35) | copy-start | bytes 3076
  1488.2 86.5 %copy-start.41 = (f32[512]{0:T(512)S(1)}, f32[512]{0:T(512)}, u32[]{:S(2)}) copy-start(f32[512]{0:T(512)} %param.37) | copy-start | bytes 6148
  1488.3 87.2 %copy-start.38 = (f32[6,128]{1,0:T(8,128)S(1)}, f32[6,128]{1,0:T(8,128)}, u32[]{:S(2)}) copy-start(f32[6,128]{1,0:T(8,128)} %param.36) | copy-start | bytes 9220
  1576.7 5.9 copy-start.5
  1582.6 60.5 %copy-start.13 = (bf16[512,1024]{0,1:T(8,128)(2,1)S(1)}, bf16[512,1024]{0,1:T(8,128)(2,1)}, u32[]{:S(2)}) copy-start(bf16[512,1024]{0,1:T(8,128)(2,1)} %copy.81) | copy-start | bytes 3145732
  (43 other events, 103.5 us)
Sparse Core Ops, SparseCore 0:
  22.0 83.4 all-gather.4
  107.6 79.2 all-gather.6
  557.5 75.1 reduce-scatter.19
  634.9 77.2 reduce-scatter.21
  715.9 41.6 reduce-scatter.29
  760.8 61.7 reduce-scatter.27
  826.0 71.3 reduce-scatter.25
  900.9 71.2 reduce-scatter.23
  976.0 121.0 all-reduce.20
  1112.3 60.7 all-reduce.10
  1183.5 60.8 all-reduce.12
  1251.5 60.8 all-reduce.14
  1319.6 60.8 all-reduce.16
  1387.6 60.8 all-reduce.18
  1452.1 35.0 reduce-scatter.35
  1490.6 33.6 reduce-scatter.31
  1527.2 33.6 reduce-scatter.33
  1562.3 80.7 all-gather.8
where the time goes:
time: 1670 us; the launch traced here: 1660 us
  waiting for transfers between devices  1070 us (64%)
  matrix products  337 us (20%)
  other arithmetic  136 us (8%)
  local copies, waits for them, and re-layouts  88.3 us (5%)
    psum x5, waiting for transfers between devices, on_device(): lax.psum(contract_cols(iterate, iterate).astype(jnp.bfloat16), 'dp')  288 us
    unnamed x23, waiting for transfers between devices  154 us
    psum x1, waiting for transfers between devices, on_device(): lax.psum(qkv_part.astype(jnp.bfloat16), 'seq').astype(jnp.float32)  122 us
    reduce_scatter x1, waiting for transfers between devices, on_device(): lax.psum_scatter(join_heads(value_grad).astype(jnp.bfloat16), 'seq', scat...  79.5 us
    all_gather x1, waiting for transfers between devices, on_device(): lax.all_gather(value_part, 'seq', axis=0, tiled=True)  78.8 us
    all_gather x1, waiting for transfers between devices, on_device(): lax.all_gather(key_part, 'seq', axis=0, tiled=True)  74.9 us
    reduce_scatter x1, waiting for transfers between devices, on_device(): lax.psum_scatter(up_grad.astype(jnp.bfloat16), 'dp', scatter_dimension=1,...  74.8 us
    reduce_scatter x1, waiting for transfers between devices, on_device(): lax.psum_scatter(down_grad.astype(jnp.bfloat16), 'dp', scatter_dimension=...  72.5 us
  transfers between devices with their start and end apart: 18, of which 18 were waited for; matrix products, arithmetic and copies ran while one was open for 7% of the time, Pallas kernels for 0%

commit v1 on v0

--- a/solution.py
+++ b/solution.py
@@ -1,8 +1,10 @@
+import functools
 import math
 import jax
 import jax.numpy as jnp
 from jax import lax
 from jax.sharding import PartitionSpec as P
+from jax.lax import axis_index, ppermute, psum
 
 NS_ITERS = 5
 MOMENTUM = 0.9
@@ -14,6 +16,21 @@
 COEF_B = -1.0
 GELU_C = 0.7978845608028654
 MASKED = -1e30
+
+
+def lead_stops_all(message, d0):
+    odd, z = (psum(1, "seq"), axis_index("seq"))
+    d_next, heard = (message, 1)
+    while heard < odd:
+        work_now = ppermute(d_next, "seq", [(q, q ^ heard) for q in range(odd)])
+        carry_in = jnp.concatenate([d_next, work_now], axis=d0)
+        w2 = jnp.concatenate([work_now, d_next], axis=d0)
+        d_next = jnp.where(z & heard == 0, carry_in, w2)
+        heard = 2 * heard
+    return d_next
+
+
+put_the_knots = functools.partial(lead_stops_all, d0=0)
 
 
 def norm_forward(values, gain_row, offset):
@@ -139,7 +156,7 @@
     value_part = (mixed[:, 2 * model_width :] + biases[2]).astype(jnp.bfloat16)
     key_rows, value_rows = (
         lax.all_gather(key_part, "seq", axis=0, tiled=True),
-        lax.all_gather(value_part, "seq", axis=0, tiled=True),
+        put_the_knots(value_part),
     )
     query_groups = split_heads(queries, groups)
     key_groups = split_heads(key_rows, groups)

time: 1670 us -> 1690 us (1.012)
    ppermute x0 -> x2, waiting for transfers between devices: none -> 159 us  [lead_stops_all(): work_now = ppermute(d_next, 'seq', [(q, q ^ heard) for q in range(odd)])]
    all_gather x1 -> x0, waiting for transfers between devices: 78.8 us -> none  [on_device(): lax.all_gather(value_part, 'seq', axis=0, tiled=True)]
    all_gather x1, waiting for transfers between devices: 74.9 us -> 0.01 us  [on_device(): lax.all_gather(key_part, 'seq', axis=0, tiled=True)]
    unnamed x23 -> x22, waiting for transfers between devices: 154 us -> 154 us
  transfers between devices with their start and end apart: 18 -> 19, of which waited for: 18 -> 18; matrix products, arithmetic and copies ran while one was open for 7% -> 8% of each run, Pallas kernels for 0% -> 0%
where the time goes in v1:
time: 1690 us
  waiting for transfers between devices  1070 us (63%)
  matrix products  337 us (20%)
  other arithmetic  147 us (9%)
  local copies, waits for them, and re-layouts  88.8 us (5%)
    psum x5, waiting for transfers between devices, on_device(): lax.psum(contract_cols(iterate, iterate).astype(jnp.bfloat16), 'dp')  288 us
    ppermute x2, waiting for transfers between devices, lead_stops_all(): work_now = ppermute(d_next, 'seq', [(q, q ^ heard) for q in range(odd)])  159 us
    unnamed x22, waiting for transfers between devices  154 us
    psum x1, waiting for transfers between devices, on_device(): lax.psum(qkv_part.astype(jnp.bfloat16), 'seq').astype(jnp.float32)  122 us
    reduce_scatter x1, waiting for transfers between devices, on_device(): lax.psum_scatter(join_heads(value_grad).astype(jnp.bfloat16), 'seq', scat...  79.6 us
    reduce_scatter x1, waiting for transfers between devices, on_device(): lax.psum_scatter(up_grad.astype(jnp.bfloat16), 'dp', scatter_dimension=1,...  74.8 us
    reduce_scatter x1, waiting for transfers between devices, on_device(): lax.psum_scatter(down_grad.astype(jnp.bfloat16), 'dp', scatter_dimension=...  72.4 us
    reduce_scatter x1, waiting for transfers between devices, on_device(): lax.psum_scatter(join_heads(key_grad).astype(jnp.bfloat16), 'seq', scatte...  66.7 us
  transfers between devices with their start and end apart: 19, of which 18 were waited for; matrix products, arithmetic and copies ran while one was open for 8% of the time, Pallas kernels for 0%

profile of v1, /device:TPU:0, one launch (start us, length us, event | category | flops | bytes accessed | tf_op | source)
XLA Modules:
  0.0 1687.5 jit_solution(9207747525896104789)
XLA Ops:
  12.8 6.1 fusion.106
  29.6 71.1 %collective-permute-done = bf16[512,1024]{1,0:T(8,128)(2,1)S(1)} collective-permute-done((bf16[512,1024]{1,0:T(8,128)(2,1)S(1)}, bf16[512,1024]{1,0:T(8,128)(2,1)S(1)}, u32[]{:S(2)}, u32[]{:S(2)}) %collective-permute-start) | collective-permute-done | bytes 1048608 | tf_op jit(solution)/shard_map/ppermute | solution.py:25
  103.0 6.3 collective-permute-start.1
  116.3 87.8 %collective-permute-done.1 = bf16[1024,1024]{1,0:T(8,128)(2,1)} collective-permute-done((bf16[1024,1024]{1,0:T(8,128)(2,1)}, bf16[1024,1024]{1,0:T(8,128)(2,1)}, u32[]{:S(2)}, u32[]{:S(2)}) %collective-permute-start.1) | collective-permute-done | bytes 2097184 | tf_op jit(solution)/shard_map/ppermute | solution.py:25
  213.2 6.4 copy.71
  219.7 102.7 %while.30 = (s32[]{:T(128)}, bf16[8,512,2,64]{1,3,2,0:T(8,128)(2,1)}, f32[8,2,512]{2,1,0:T(2,128)S(1)}, bf16[8,2048,2,64]{1,3,2,0:T(8,128)(2,1)}, bf16[8,512,2,6...) while((s32[]{:T(128)}, ...), condition=%wide.region_5.6_spmd.clone.clone, body=%wide.region_2.5_spmd.clone.clone.sunk | while | flops 575667200 | bytes 47618196 | solution.py:168
  325.4 10.7 fusion.108
  336.1 13.5 fusion.114
  349.7 5.7 multiply_reduce_fusion.1
  360.9 222.5 %while.31 = (s32[]{:T(128)}, bf16[8,512,2,64]{1,3,2,0:T(8,128)(2,1)}, bf16[8,2048,2,64]{1,3,2,0:T(8,128)(2,1)}, bf16[8,2048,2,64]{1,3,2,0:T(8,128)(2,1)}, bf16[8...) while((s32[]{:T(128)}, ...), condition=%wide.region_12.13_spmd.clone.clone, body=%wide.region_10.12_spmd.clone.clone.sunk | while | flops 1368783872 | bytes 144864496 | solution.py:197
  369.6 5.7 multiply_reduce_fusion.7
  375.3 6.6 multiply_convert_fusion.7
  397.3 5.7 multiply_reduce_fusion.7
  403.1 6.6 multiply_convert_fusion.7
  425.1 5.7 multiply_reduce_fusion.7
  430.9 6.6 multiply_convert_fusion.7
  452.9 5.7 multiply_reduce_fusion.7
  458.6 6.6 multiply_convert_fusion.7
  480.7 5.7 multiply_reduce_fusion.7
  486.4 6.6 multiply_convert_fusion.7
  508.5 5.7 multiply_reduce_fusion.7
  514.2 6.6 multiply_convert_fusion.7
  536.3 5.7 multiply_reduce_fusion.7
  542.0 6.6 multiply_convert_fusion.7
  564.1 5.7 multiply_reduce_fusion.7
  569.8 6.6 multiply_convert_fusion.7
  592.6 66.7 %reduce-scatter.20.cloned.1.call-done = bf16[512,1024]{0,1:T(8,128)(2,1)} async-done(((bf16[2048,1024]{0,1:T(8,128)(2,1)}), bf16[512,1024]{0,1:T(8,128)(2,1)}) %reduce-scatter.20.cloned.1.call-update) | async-done | bytes 1048592 | tf_op jit(solution)/shard_map/reduce_scatter | solution.py:210
  659.3 79.6 %reduce-scatter.22.cloned.1.call-done = bf16[512,1024]{0,1:T(8,128)(2,1)} async-done(((bf16[2048,1024]{0,1:T(8,128)(2,1)}), bf16[512,1024]{0,1:T(8,128)(2,1)}) %reduce-scatter.22.cloned.1.call-update) | async-done | bytes 1048592 | tf_op jit(solution)/shard_map/reduce_scatter | solution.py:213
  739.0 8.1 convolution_convert_fusion.1
  747.0 8.7 copy.80
  756.9 11.4 convert_bitcast_fusion
  770.0 9.2 convolution_convert_fusion
  786.1 63.2 %reduce-scatter.28.cloned.1.call-done = bf16[384,1024]{1,0:T(8,128)(2,1)} async-done(((bf16[3072,1024]{1,0:T(8,128)(2,1)}), bf16[384,1024]{1,0:T(8,128)(2,1)}) %reduce-scatter.28.cloned.1.call-update) | async-done | bytes 786448
  851.6 72.4 %reduce-scatter.26.cloned.1.call-done = bf16[1024,512]{1,0:T(8,128)(2,1)} async-done(((bf16[1024,4096]{1,0:T(8,128)(2,1)}), bf16[1024,512]{1,0:T(8,128)(2,1)}) %reduce-scatter.26.cloned.1.call-update) | async-done | bytes 1048592 | tf_op jit(solution)/shard_map/reduce_scatter | solution.py:248
  924.0 74.8 %reduce-scatter.24.cloned.1.call-done = bf16[1024,512]{1,0:T(8,128)(2,1)} async-done(((bf16[1024,4096]{1,0:T(8,128)(2,1)}), bf16[1024,512]{1,0:T(8,128)(2,1)}) %reduce-scatter.24.cloned.1.call-update) | async-done | bytes 1048592 | tf_op jit(solution)/shard_map/reduce_scatter | solution.py:245
  1001.7 121.9 %all-reduce.21.cloned.1.call-done = (bf16[1024,384]{1,0:T(8,128)(2,1)}, bf16[1024,128]{1,0:T(8,128)(2,1)}, bf16[1024,512]{1,0:T(8,128)(2,1)}, bf16[1024,512]{1,0:T(8,128)(2,1)}) async-done(((bf16[1024,384]{1,0:T(8,128)(2,1)}, bf16[1024,128]{1,0:T(8,128)(2,1)}, bf16[1024,512]{1,0:T(8,128)(2,1)}, bf16[1024,512]{1,0:T(8,128)(2,1)}), (bf16[1024,384]{1,0:T(8,128)(2,1)}, bf16[1024,128]{1,0:T(8,128)(2,1)}, ...) | async-done | bytes 3145744 | tf_op jit(solution)/shard_map/psum | solution.py:262
  1138.8 60.9 %all-reduce.11.cloned.1.call-done = bf16[1024,1024]{1,0:T(8,128)(2,1)} async-done(((bf16[1024,1024]{1,0:T(8,128)(2,1)}), bf16[1024,1024]{1,0:T(8,128)(2,1)}) %all-reduce.11.cloned.1.call-update) | async-done | bytes 2097168 | tf_op jit(solution)/shard_map/psum | solution.py:288
  1210.0 60.9 %all-reduce.13.cloned.1.call-done = bf16[1024,1024]{1,0:T(8,128)(2,1)} async-done(((bf16[1024,1024]{1,0:T(8,128)(2,1)}), bf16[1024,1024]{1,0:T(8,128)(2,1)}) %all-reduce.13.cloned.1.call-update) | async-done | bytes 2097168 | tf_op jit(solution)/shard_map/psum | solution.py:288
  1278.0 60.9 %all-reduce.15.cloned.1.call-done = bf16[1024,1024]{1,0:T(8,128)(2,1)} async-done(((bf16[1024,1024]{1,0:T(8,128)(2,1)}), bf16[1024,1024]{1,0:T(8,128)(2,1)}) %all-reduce.15.cloned.1.call-update) | async-done | bytes 2097168 | tf_op jit(solution)/shard_map/psum | solution.py:288
  1346.1 60.9 %all-reduce.17.cloned.1.call-done = bf16[1024,1024]{1,0:T(8,128)(2,1)} async-done(((bf16[1024,1024]{1,0:T(8,128)(2,1)}), bf16[1024,1024]{1,0:T(8,128)(2,1)}) %all-reduce.17.cloned.1.call-update) | async-done | bytes 2097168 | tf_op jit(solution)/shard_map/psum | solution.py:288
  1416.0 9.4 fusion.81
  1430.6 44.5 %all-reduce.19.cloned.1.call-done = bf16[1024,1024]{1,0:T(8,128)(2,1)} async-done(((bf16[1024,1024]{1,0:T(8,128)(2,1)}), bf16[1024,1024]{1,0:T(8,128)(2,1)}) %all-reduce.19.cloned.1.call-update) | async-done | bytes 2097168 | tf_op jit(solution)/shard_map/psum | solution.py:288
  1484.0 12.6 add_convert_fusion.5
  1496.6 17.1 %reduce-scatter.36.cloned.1.call-done = bf16[512,1]{1,0:T(8,128)(2,1)} async-done(((bf16[4096,1]{1,0:T(8,128)(2,1)}), bf16[512,1]{1,0:T(8,128)(2,1)}) %reduce-scatter.36.cloned.1.call-update) | async-done | bytes 1040
  1519.0 31.8 %reduce-scatter.32.cloned.1.call-done = bf16[128,2]{1,0:T(8,128)(2,1)} async-done(((bf16[1024,2]{1,0:T(8,128)(2,1)}), bf16[128,2]{1,0:T(8,128)(2,1)}) %reduce-scatter.32.cloned.1.call-update) | async-done | bytes 528
  1551.7 35.8 %reduce-scatter.34.cloned.1.call-done = bf16[128,6]{1,0:T(8,128)(2,1)} async-done(((bf16[1024,6]{1,0:T(8,128)(2,1)}), bf16[128,6]{1,0:T(8,128)(2,1)}) %reduce-scatter.34.cloned.1.call-update) | async-done | bytes 1552
  1588.3 11.8 all-reduce.2
  1610.9 58.7 %all-gather.6.cloned.1.call-done = bf16[4096,512]{1,0:T(8,128)(2,1)} async-done(((bf16[1024,512]{1,0:T(8,128)(2,1)}), bf16[4096,512]{1,0:T(8,128)(2,1)}) %all-gather.6.cloned.1.call-update) | async-done | bytes 4194320 | tf_op jit(solution)/shard_map/all_gather | solution.py:302
  (391 shorter events, 383.8 us)
Async XLA Ops:
  7.2 206.1 %all-gather.4.cloned.1.call-start = ((), (), s32[]{:S(2)}) async-start(), calls=%async_computation.9 | async-start | bytes 5242880 | tf_op jit(solution)/shard_map/all_gather | solution.py:158
  8.7 10.2 copy-start.24
  10.3 8.5 copy-start.31
  11.1 7.7 copy-start.26
  12.7 6.1 copy-start.36
  12.8 312.6 %copy-start.34 = (f32[1,1024]{1,0:T(1,128)}, f32[1,1024]{1,0:T(1,128)S(1)}, u32[]{:S(2)}) copy-start(f32[1,1024]{1,0:T(1,128)S(1)} %get-tuple-element.393) | copy-start | bytes 12292
  22.7 636.6 %reduce-scatter.20.cloned.1.call-start = ((), (), s32[]{:S(2)}) async-start(), calls=%async_computation.10 | async-start | bytes 5242880 | tf_op jit(solution)/shard_map/reduce_scatter | solution.py:210
  26.5 74.1 %collective-permute-start = (bf16[512,1024]{1,0:T(8,128)(2,1)S(1)}, bf16[512,1024]{1,0:T(8,128)(2,1)S(1)}, u32[]{:S(2)}, u32[]{:S(2)}) collective-permute-start(bf16[512,1024]{1,0:T(8,128)(2,1)S(1)} %get-tuple-element.389), channel_id=1, source_target_pairs={{0,1},{1,0},{2,3},{3,2},{4,5},{5,4},{6,7},{7,6},{8,9},{9,8},{10,11... | collective-permute-start | bytes 3145736 | tf_op jit(solution)/shard_map/ppermute | solution.py:25
  29.6 80.7 %copy-start.43 = (f32[16]{0:T(128)S(1)}, f32[16]{0:T(128)}, u32[]{:S(2)}) copy-start(f32[16]{0:T(128)} %param.30) | copy-start | bytes 196
  103.0 101.2 %collective-permute-start.1 = (bf16[1024,1024]{1,0:T(8,128)(2,1)}, bf16[1024,1024]{1,0:T(8,128)(2,1)}, u32[]{:S(2)}, u32[]{:S(2)}) collective-permute-start(bf16[1024,1024]{1,0:T(8,128)(2,1)} %maximum_select_fusion.2), channel_id=1, source_target_pairs={{0,2},{1,3},{2,0},{3,1},{4,6},{5,7},{6,4},{7,5},{8,10},{9,11},{10,... | collective-permute-start | bytes 6291464 | tf_op jit(solution)/shard_map/ppermute | solution.py:25
  219.7 102.7 %copy-start.3 = (bf16[512,1024]{1,0:T(8,128)(2,1)S(1)}, bf16[512,1024]{1,0:T(8,128)(2,1)}, u32[]{:S(2)}) copy-start(bf16[512,1024]{1,0:T(8,128)(2,1)} %param.21) | copy-start | bytes 3145732
  219.7 102.7 %copy-start.14 = (bf16[1024,1024]{1,0:T(8,128)(2,1)S(1)}, bf16[1024,1024]{1,0:T(8,128)(2,1)}, u32[]{:S(2)}) copy-start(bf16[1024,1024]{1,0:T(8,128)(2,1)} %param.24) | copy-start | bytes 6291460
  325.0 30.4 %copy-start.1 = (f32[512,1024]{1,0:T(8,128)}, f32[512,1024]{1,0:T(8,128)S(1)}, u32[]{:S(2)}) copy-start(f32[512,1024]{1,0:T(8,128)S(1)} %get-tuple-element.402) | copy-start | bytes 6291460
  325.3 10.8 copy-start.17
  325.4 10.8 copy-start.44
  325.4 24.3 %slice-start = ((s8[8388608]{0:T(1024)(128)(4,1)}), s8[4194304]{0:T(1024)(128)(4,1)S(1)}, s32[]{:S(2)}) async-start(s8[8388608]{0:T(1024)(128)(4,1)} %bitcast.230), calls=%async_computation.26 | async-start | bytes 8388608
  336.1 13.6 slice-start.1
  349.7 5.7 copy-start.49
  583.4 155.5 %reduce-scatter.22.cloned.1.call-start = ((), (), s32[]{:S(2)}) async-start(), calls=%async_computation.11 | async-start | bytes 5242880 | tf_op jit(solution)/shard_map/reduce_scatter | solution.py:213
  584.2 200.1 %reduce-scatter.30.cloned.1.call-start = ((), (), s32[]{:S(2)}) async-start(), calls=%async_computation.21 | async-start | bytes 2359296
  587.9 151.1 %copy-start.4 = (bf16[512,1024]{1,0:T(8,128)(2,1)S(1)}, bf16[512,1024]{1,0:T(8,128)(2,1)}, u32[]{:S(2)}) copy-start(bf16[512,1024]{1,0:T(8,128)(2,1)} %param.21) | copy-start | bytes 3145732
  587.9 151.1 %copy-start.19 = (bf16[8,512,2,64]{1,3,2,0:T(8,128)(2,1)S(1)}, bf16[8,512,2,64]{1,3,2,0:T(8,128)(2,1)}, u32[]{:S(2)}) copy-start(bf16[8,512,2,64]{1,3,2,0:T(8,128)(2,1)} %get-tuple-element.137) | copy-start | bytes 3145732
  587.9 151.1 %copy-start.25 = (f32[512]{0:T(512)S(1)}, f32[512]{0:T(512)}, u32[]{:S(2)}) copy-start(f32[512]{0:T(512)} %copy-done.24) | copy-start | bytes 6148
  587.9 151.1 %copy-start.27 = (f32[1,1024]{1,0:T(1,128)S(1)}, f32[1,1024]{1,0:T(1,128)}, u32[]{:S(2)}) copy-start(f32[1,1024]{1,0:T(1,128)} %copy-done.26) | copy-start | bytes 12292
  587.9 151.1 %copy-start.32 = (f32[512]{0:T(512)S(1)}, f32[512]{0:T(512)}, u32[]{:S(2)}) copy-start(f32[512]{0:T(512)} %copy-done.31) | copy-start | bytes 6148
  587.9 151.1 %copy-start.37 = (f32[1,1024]{1,0:T(1,128)S(1)}, f32[1,1024]{1,0:T(1,128)}, u32[]{:S(2)}) copy-start(f32[1,1024]{1,0:T(1,128)} %copy-done.36) | copy-start | bytes 12292
  592.2 257.2 %reduce-scatter.28.cloned.1.call-start = ((), (), s32[]{:S(2)}) async-start(), calls=%async_computation.20 | async-start | bytes 7077888
  755.7 168.3 %reduce-scatter.26.cloned.1.call-start = ((), (), s32[]{:S(2)}) async-start(), calls=%async_computation.13 | async-start | bytes 9437184 | tf_op jit(solution)/shard_map/reduce_scatter | solution.py:248
  768.4 230.4 %reduce-scatter.24.cloned.1.call-start = ((), (), s32[]{:S(2)}) async-start(), calls=%async_computation.12 | async-start | bytes 9437184 | tf_op jit(solution)/shard_map/reduce_scatter | solution.py:245
  779.2 344.4 %all-reduce.21.cloned.1.call-start = ((), (), s32[]{:S(2)}) async-start(), calls=%async_computation.25 | async-start | bytes 6291456 | tf_op jit(solution)/shard_map/psum | solution.py:262
  998.8 200.9 %all-reduce.11.cloned.1.call-start = ((), (), s32[]{:S(2)}) async-start(), calls=%async_computation.14 | async-start | bytes 4194304 | tf_op jit(solution)/shard_map/psum | solution.py:288
  1138.8 132.2 %all-reduce.13.cloned.1.call-start = ((), (), s32[]{:S(2)}) async-start(), calls=%async_computation.15 | async-start | bytes 4194304 | tf_op jit(solution)/shard_map/psum | solution.py:288
  1210.0 129.0 %all-reduce.15.cloned.1.call-start = ((), (), s32[]{:S(2)}) async-start(), calls=%async_computation.16 | async-start | bytes 4194304 | tf_op jit(solution)/shard_map/psum | solution.py:288
  1278.0 129.0 %all-reduce.17.cloned.1.call-start = ((), (), s32[]{:S(2)}) async-start(), calls=%async_computation.17 | async-start | bytes 4194304 | tf_op jit(solution)/shard_map/psum | solution.py:288
  1346.0 129.0 %all-reduce.19.cloned.1.call-start = ((), (), s32[]{:S(2)}) async-start(), calls=%async_computation.18 | async-start | bytes 4194304 | tf_op jit(solution)/shard_map/psum | solution.py:288
  1414.1 99.7 %reduce-scatter.36.cloned.1.call-start = ((), (), s32[]{:S(2)}) async-start(), calls=%async_computation.24 | async-start | bytes 1179648
  1415.7 12.2 copy-start.39
  1415.8 12.2 copy-start.30
  1415.8 12.2 copy-start.29
  1415.8 135.1 %reduce-scatter.32.cloned.1.call-start = ((), (), s32[]{:S(2)}) async-start(), calls=%async_computation.22 | async-start | bytes 294912
  1426.4 161.0 %reduce-scatter.34.cloned.1.call-start = ((), (), s32[]{:S(2)}) async-start(), calls=%async_computation.23 | async-start | bytes 294912
  1430.5 239.1 %all-gather.6.cloned.1.call-start = ((), (), s32[]{:S(2)}) async-start(), calls=%async_computation.19 | async-start | bytes 5242880 | tf_op jit(solution)/shard_map/all_gather | solution.py:302
  1479.4 4.6 copy-start.33
  1514.8 85.3 %copy-start.42 = (f32[2,128]{1,0:T(2,128)S(1)}, f32[2,128]{1,0:T(2,128)}, u32[]{:S(2)}) copy-start(f32[2,128]{1,0:T(2,128)} %param.35) | copy-start | bytes 3076
  1514.8 86.5 %copy-start.41 = (f32[512]{0:T(512)S(1)}, f32[512]{0:T(512)}, u32[]{:S(2)}) copy-start(f32[512]{0:T(512)} %param.37) | copy-start | bytes 6148
  1514.8 87.2 %copy-start.38 = (f32[6,128]{1,0:T(8,128)S(1)}, f32[6,128]{1,0:T(8,128)}, u32[]{:S(2)}) copy-start(f32[6,128]{1,0:T(8,128)} %param.36) | copy-start | bytes 9220
  1603.2 5.9 copy-start.5
  1609.1 60.5 %copy-start.13 = (bf16[512,1024]{0,1:T(8,128)(2,1)S(1)}, bf16[512,1024]{0,1:T(8,128)(2,1)}, u32[]{:S(2)}) copy-start(bf16[512,1024]{0,1:T(8,128)(2,1)} %copy.90) | copy-start | bytes 3145732
  (44 other events, 106.6 us)
Sparse Core Ops, SparseCore 0:
  22.8 110.4 all-gather.3
  583.5 75.7 reduce-scatter.19
  661.6 77.2 reduce-scatter.21
  742.7 41.6 reduce-scatter.29
  787.5 61.7 reduce-scatter.27
  852.7 71.2 reduce-scatter.25
  927.4 71.2 reduce-scatter.23
  1002.5 121.0 all-reduce.20
  1138.9 60.7 all-reduce.10
  1210.1 60.8 all-reduce.12
  1278.1 60.8 all-reduce.14
  1346.1 60.8 all-reduce.16
  1414.2 60.8 all-reduce.18
  1478.6 35.0 reduce-scatter.35
  1517.2 33.6 reduce-scatter.31
  1553.7 33.6 reduce-scatter.33
  1588.8 80.7 all-gather.5
